TPU v7x, 32 devices: a whole 2x2x4 slice. The times are simulated.
32 devices in a mesh: wide: 16 (over z, y, core), narrow: 2 (over x).
Axes of the slice: x: 2, y: 2, z: 4, core: 2. Of those that a mesh axis runs over, the one named last changes fastest.
Arguments:
- gradient: float32 [3072, 3072], P('wide', 'narrow'), may hold values from -6 to 6
- first_moment: float32 [3072, 3072], P('wide', 'narrow'), may hold values from -6 to 6
- second_moment: float32 [3072, 3072], P('wide', 'narrow'), may hold values from 0.25 to 4
- left_basis: float32 [3072, 3072], P('wide', 'narrow'), may hold values from -0.15625 to 0.15625
- right_basis: float32 [3072, 3072], P('wide', 'narrow'), may hold values from -0.109375 to 0.109375
Outputs:
- update: float32 [3072, 3072], P('wide', 'narrow')
- new_first: float32 [3072, 3072], P('wide', 'narrow')
- new_second: float32 [3072, 3072], P('wide', 'narrow')
All inputs are finite; a program needn't handle non-finite values.
Results may differ from a plain program's by a relative error of at most 0.000075.
Values sent between devices are 32-bit elements; how exact they have to be, the bound alone decides.
A program may use at most 128 MiB of HBM per device.

v0:
```python
import jax
import jax.numpy as jnp
from jax import lax
from jax.sharding import PartitionSpec as P

STEP = 10
beta_first = 0.9
beta_second = 0.95
epsilon = 1e-08


def product(left, right):
    return jnp.dot(left, right, precision=lax.Precision.HIGHEST, preferred_element_type=jnp.float32)


def contract(left, right, left_dim, right_dim):
    return lax.dot_general(
        left,
        right,
        (((left_dim,), (right_dim,)), ((), ())),
        precision=lax.Precision.HIGHEST,
        preferred_element_type=jnp.float32,
    )


def body(gradient, first_moment, second_moment, left_basis, right_basis):
    grad_rows, left_rows = (
        lax.all_gather(gradient, "narrow", axis=1, tiled=True),
        lax.all_gather(left_basis, "narrow", axis=1, tiled=True),
    )
    columns = grad_rows
    rotated_right = product(columns, lax.all_gather(right_basis, "wide", axis=0, tiled=True))
    columns = left_rows
    rotated = lax.psum_scatter(
        contract(columns, rotated_right, 0, 0), "wide", scatter_dimension=0, tiled=True
    )
    new_first = beta_first * first_moment + (1.0 - beta_first) * rotated
    new_second = beta_second * second_moment + (1.0 - beta_second) * rotated * rotated
    direction = (
        new_first
        / (1.0 - beta_first**STEP)
        / (jnp.sqrt(new_second / (1.0 - beta_second**STEP)) + epsilon)
    )
    columns = left_rows
    back_left = product(columns, lax.all_gather(direction, "wide", axis=0, tiled=True))
    terms = contract(back_left, lax.all_gather(right_basis, "wide", axis=0, tiled=True), 1, 1)
    update = lax.psum_scatter(terms, "narrow", scatter_dimension=1, tiled=True)
    return (update, new_first, new_second)


def solution(mesh):
    placed = (
        P("wide", "narrow"),
        P("wide", "narrow"),
        P("wide", "narrow"),
        P("wide", "narrow"),
        P("wide", "narrow"),
    )
    return jax.shard_map(
        body,
        mesh=mesh,
        in_specs=placed,
        out_specs=(P("wide", "narrow"), P("wide", "narrow"), P("wide", "narrow")),
        check_vma=False,
    )
```

profile of v0, /device:TPU:0, one launch (start us, length us, event | category | flops | bytes accessed | tf_op | source)
XLA Modules:
  0.0 637.2 jit_solution(4374816837675824320)
XLA Ops:
  7.2 0.0 all-gather.5.cloned.1.call-start
  7.2 0.7 all-gather.5.cloned.1.call-update
  7.9 0.0 all-gather.7.cloned.1.call-start
  7.9 0.7 all-gather.7.cloned.1.call-update
  8.6 0.0 all-gather.9.cloned.1.call-start
  8.7 0.7 all-gather.9.cloned.1.call-update
  9.4 0.0 reduce-scatter.7.cloned.1.call-start
  9.4 38.9 %all-gather.5.cloned.1.call-done = f32[192,3072]{1,0:T(8,128)} async-done(((f32[192,1536]{1,0:T(8,128)}), f32[192,3072]{1,0:T(8,128)}) %all-gather.5.cloned.1.call-update) | async-done | bytes 2359312 | tf_op jit(solution)/shard_map/all_gather | solution.py:28
  48.3 100.5 %all-gather.7.cloned.1.call-done = f32[3072,1536]{1,0:T(8,128)} async-done(((f32[192,1536]{1,0:T(8,128)}), f32[3072,1536]{1,0:T(8,128)}) %all-gather.7.cloned.1.call-update) | async-done | bytes 18874384 | tf_op jit(solution)/shard_map/all_gather | solution.py:32
  148.8 16.6 %fusion.2 = f32[192,1536]{1,0:T(8,128)S(1)} fusion(f32[192,3072]{1,0:T(8,128)} %all-gather.5.cloned.1.call-done, f32[3072,1536]{1,0:T(8,128)} %all-gather.7.cloned.1.call-done), kind=kOutput, calls=%fused_computation.5 | convolution fusion | flops 10871635968 | bytes 22413312 | tf_op jit(solution)/shard_map/dot_general | solution.py:13
  165.5 21.0 %all-gather.9.cloned.1.call-done = f32[192,3072]{1,0:T(8,128)} async-done(((f32[192,1536]{1,0:T(8,128)}), f32[192,3072]{1,0:T(8,128)}) %all-gather.9.cloned.1.call-update) | async-done | bytes 2359312 | tf_op jit(solution)/shard_map/all_gather | solution.py:29
  186.5 19.5 %convolution_bitcast_fusion = f32[3072,1536]{0,1:T(8,128)} fusion(f32[192,1536]{1,0:T(8,128)S(1)} %fusion.2, f32[192,3072]{1,0:T(8,128)} %all-gather.9.cloned.1.call-done), kind=kOutput, calls=%fused_computation | convolution fusion | flops 10871635968 | bytes 22413312 | tf_op jit(solution)/shard_map/dot_general | solution.py:17
  206.0 18.7 %copy.17 = f32[3072,1536]{1,0:T(8,128)} copy(f32[3072,1536]{0,1:T(8,128)} %convolution_bitcast_fusion) | data formatting | bytes 37748736
  224.7 0.0 copy-start.3
  224.7 0.0 reduce-scatter.7.cloned.1.call-update
  224.7 0.2 all-gather.11.cloned.1.call-start
  225.0 1.0 copy-done.3
  226.0 0.5 copy.12
  226.4 1.7 copy.13
  228.2 190.7 %reduce-scatter.7.cloned.1.call-done = f32[192,1536]{1,0:T(8,128)} async-done(((f32[3072,1536]{1,0:T(8,128)}), f32[192,1536]{1,0:T(8,128)}) %reduce-scatter.7.cloned.1.call-update) | async-done | bytes 1179664
  418.9 3.0 copy.18
  421.9 4.1 add_divide_fusion
  426.0 0.0 copy-start
  426.0 3.0 copy.14
  429.0 0.0 all-gather.11.cloned.1.call-update
  429.1 0.0 reduce-scatter.5.cloned.1.call-start
  429.1 98.1 %all-gather.11.cloned.1.call-done = f32[3072,1536]{1,0:T(8,128)} async-done(((f32[192,1536]{1,0:T(8,128)}), f32[3072,1536]{1,0:T(8,128)}) %all-gather.11.cloned.1.call-update) | async-done | bytes 18874384 | tf_op jit(solution)/shard_map/all_gather | solution.py:45
  527.2 0.0 copy-done
  527.2 32.5 %fusion.3 = f32[1536,192]{1,0:T(8,128)S(1)} fusion(f32[3072,1536]{1,0:T(8,128)} %all-gather.11.cloned.1.call-done, f32[192,3072]{1,0:T(8,128)S(1)} %copy-done), kind=kOutput, calls=%fused_computation.6 | convolution fusion | flops 10871635968 | bytes 22413312 | tf_op jit(solution)/shard_map/dot_general | solution.py:13
  559.8 35.7 %fusion.4 = f32[192,3072]{1,0:T(8,128)} fusion(f32[1536,192]{1,0:T(8,128)S(1)} %fusion.3, f32[3072,1536]{1,0:T(8,128)} %all-gather.7.cloned.1.call-done), kind=kOutput, calls=%fused_computation.7 | convolution fusion | flops 10871635968 | bytes 22413312 | tf_op jit(solution)/shard_map/dot_general | solution.py:17
  595.4 0.0 copy-start.2
  595.4 0.0 reduce-scatter.5.cloned.1.call-update
  595.5 0.0 copy-start.1
  595.5 1.4 copy-done.2
  596.8 1.5 copy.15
  598.3 0.0 copy-done.1
  598.3 1.5 copy.16
  599.8 30.6 %reduce-scatter.5.cloned.1.call-done = f32[192,1536]{1,0:T(8,128)} async-done(((f32[192,3072]{1,0:T(8,128)}), f32[192,1536]{1,0:T(8,128)}) %reduce-scatter.5.cloned.1.call-update) | async-done | bytes 1179664 | tf_op jit(solution)/shard_map/reduce_scatter | solution.py:47
Async XLA Ops:
  7.2 41.2 %all-gather.5.cloned.1.call-start = ((), (), s32[]{:S(2)}) async-start(), calls=%async_computation.2 | async-start | bytes 3538944 | tf_op jit(solution)/shard_map/all_gather | solution.py:28
  7.9 140.9 %all-gather.7.cloned.1.call-start = ((), (), s32[]{:S(2)}) async-start(), calls=%async_computation.3 | async-start | bytes 20054016 | tf_op jit(solution)/shard_map/all_gather | solution.py:32
  8.6 177.8 %all-gather.9.cloned.1.call-start = ((), (), s32[]{:S(2)}) async-start(), calls=%async_computation.4 | async-start | bytes 3538944 | tf_op jit(solution)/shard_map/all_gather | solution.py:29
  9.4 409.5 %reduce-scatter.7.cloned.1.call-start = ((), (), s32[]{:S(2)}) async-start(), calls=%async_computation.7 | async-start | bytes 20054016
  224.7 1.3 copy-start.3
  224.7 302.5 %all-gather.11.cloned.1.call-start = ((), (), s32[]{:S(2)}) async-start(), calls=%async_computation.5 | async-start | bytes 20054016 | tf_op jit(solution)/shard_map/all_gather | solution.py:45
  426.0 101.2 %copy-start = (f32[192,3072]{1,0:T(8,128)S(1)}, f32[192,3072]{1,0:T(8,128)}, u32[]{:S(2)}) copy-start(f32[192,3072]{1,0:T(8,128)} %all-gather.9.cloned.1.call-done) | copy-start | bytes 7077892
  429.1 201.3 %reduce-scatter.5.cloned.1.call-start = ((), (), s32[]{:S(2)}) async-start(), calls=%async_computation.6 | async-start | bytes 3538944 | tf_op jit(solution)/shard_map/reduce_scatter | solution.py:47
  595.4 1.4 copy-start.2
  595.5 2.9 copy-start.1
Sparse Core Ops, SparseCore 0:
  9.5 38.7 all-gather.4
  49.9 98.8 all-gather.6
  150.4 36.0 all-gather.8
  224.9 194.0 reduce-scatter.6
  429.2 98.0 all-gather.10
  595.6 34.7 reduce-scatter.4
where the time goes:
time: 638 us; the launch traced here: 637 us
  waiting for transfers between devices  482 us (76%)
  matrix products  104 us (16%)
  local copies, waits for them, and re-layouts  32.2 us (5%)
  between operations  14.2 us (2%)
    unnamed x7, waiting for transfers between devices  193 us
    all_gather x1, waiting for transfers between devices, body(): lax.all_gather(right_basis, 'wide', axis=0, tiled=True)  101 us
    all_gather x1, waiting for transfers between devices, body(): lax.all_gather(direction, 'wide', axis=0, tiled=True)  98.1 us
    dot_general x2, matrix products, contract(): lax.dot_general(left, right, (((left_dim,), (right_dim,)), ((), ())), pre...  55.2 us
    dot_general x2, matrix products, product(): jnp.dot(left, right, precision=lax.Precision.HIGHEST, preferred_element_t...  49.1 us
    all_gather x1, waiting for transfers between devices, body(): lax.all_gather(gradient, 'narrow', axis=1, tiled=True)  38.9 us
    reduce_scatter x1, waiting for transfers between devices, body(): update = lax.psum_scatter(terms, 'narrow', scatter_dimension=1, tiled=True)  30.6 us
    unnamed x14, local copies, waits for them, and re-layouts  29.2 us
  transfers between devices with their start and end apart: 6, of which 6 were waited for; matrix products, arithmetic and copies ran while one was open for 3% of the time, Pallas kernels for 0%

commit v1 on v0

--- a/solution.py
+++ b/solution.py
@@ -2,6 +2,7 @@
 import jax.numpy as jnp
 from jax import lax
 from jax.sharding import PartitionSpec as P
+from jax.lax import all_gather
 
 STEP = 10
 beta_first = 0.9
@@ -24,8 +25,13 @@
 
 
 def body(gradient, first_moment, second_moment, left_basis, right_basis):
+
+    def measure_edges(inputs):
+        v_next = all_gather(inputs, "narrow")
+        return jnp.concatenate(v_next, axis=1)
+
     grad_rows, left_rows = (
-        lax.all_gather(gradient, "narrow", axis=1, tiled=True),
+        measure_edges(gradient),
         lax.all_gather(left_basis, "narrow", axis=1, tiled=True),
     )
     columns = grad_rows

time: 638 us -> 609 us (0.955)
  matrix products: 104 us -> 75.1 us
    dot_general x2, matrix products: 49.1 us -> 32.5 us  [product(): jnp.dot(left, right, precision=lax.Precision.HIGHEST, preferred_element_t...]
    dot_general x2, matrix products: 55.2 us -> 42.6 us  [contract(): lax.dot_general(left, right, (((left_dim,), (right_dim,)), ((), ())), pre...]
    unnamed x14 -> x15, local copies, waits for them, and re-layouts: 29.2 us -> 29.6 us
  transfers between devices with their start and end apart: 6 -> 6, of which waited for: 6 -> 6; matrix products, arithmetic and copies ran while one was open for 3% -> 4% of each run, Pallas kernels for 0% -> 0%
where the time goes in v1:
time: 609 us
  waiting for transfers between devices  479 us (79%)
  matrix products  75.1 us (12%)
  local copies, waits for them, and re-layouts  36.1 us (6%)
  between operations  14.2 us (2%)
    unnamed x7, waiting for transfers between devices  193 us
    all_gather x1, waiting for transfers between devices, body(): lax.all_gather(direction, 'wide', axis=0, tiled=True)  98.1 us
    all_gather x1, waiting for transfers between devices, body(): lax.all_gather(right_basis, 'wide', axis=0, tiled=True)  96.6 us
    dot_general x2, matrix products, contract(): lax.dot_general(left, right, (((left_dim,), (right_dim,)), ((), ())), pre...  42.6 us
    all_gather x1, waiting for transfers between devices, measure_edges(): v_next = all_gather(inputs, 'narrow')  38.9 us
    dot_general x2, matrix products, product(): jnp.dot(left, right, precision=lax.Precision.HIGHEST, preferred_element_t...  32.5 us
    reduce_scatter x1, waiting for transfers between devices, body(): update = lax.psum_scatter(terms, 'narrow', scatter_dimension=1, tiled=True)  30.6 us
    unnamed x15, local copies, waits for them, and re-layouts  29.6 us
  transfers between devices with their start and end apart: 6, of which 6 were waited for; matrix products, arithmetic and copies ran while one was open for 4% of the time, Pallas kernels for 0%

profile of v1, /device:TPU:0, one launch (start us, length us, event | category | flops | bytes accessed | tf_op | source)
XLA Modules:
  0.0 608.7 jit_solution(17895347504615176625)
XLA Ops:
  7.2 0.0 all-gather.12.cloned.1.call-start
  7.2 0.7 all-gather.12.cloned.1.call-update
  7.9 0.0 all-gather.6.cloned.1.call-start
  7.9 0.7 all-gather.6.cloned.1.call-update
  8.6 0.0 all-gather.8.cloned.1.call-start
  8.7 0.7 all-gather.8.cloned.1.call-update
  9.4 0.0 reduce-scatter.7.cloned.1.call-start
  9.4 38.9 %all-gather.12.cloned.1.call-done = f32[384,1536]{1,0:T(8,128)} async-done(((f32[192,1536]{1,0:T(8,128)}), f32[384,1536]{1,0:T(8,128)}) %all-gather.12.cloned.1.call-update) | async-done | bytes 2359312 | tf_op jit(solution)/shard_map/all_gather | solution.py:30
  48.3 3.5 copy.18
  51.8 0.4 copy.25
  52.2 96.6 %all-gather.6.cloned.1.call-done = f32[3072,1536]{1,0:T(8,128)} async-done(((f32[192,1536]{1,0:T(8,128)}), f32[3072,1536]{1,0:T(8,128)}) %all-gather.6.cloned.1.call-update) | async-done | bytes 18874384 | tf_op jit(solution)/shard_map/all_gather | solution.py:38
  148.8 15.9 %fusion.2 = f32[192,1536]{1,0:T(8,128)S(1)} fusion(f32[192,3072]{1,0:T(8,128)S(1)} %bitcast.16, f32[3072,1536]{1,0:T(8,128)} %all-gather.6.cloned.1.call-done), kind=kOutput, calls=%fused_computation.5 | convolution fusion | flops 10871635968 | bytes 22413312 | tf_op jit(solution)/shard_map/dot_general | solution.py:14
  164.8 21.7 %all-gather.8.cloned.1.call-done = f32[192,3072]{1,0:T(8,128)} async-done(((f32[192,1536]{1,0:T(8,128)}), f32[192,3072]{1,0:T(8,128)}) %all-gather.8.cloned.1.call-update) | async-done | bytes 2359312 | tf_op jit(solution)/shard_map/all_gather | solution.py:35
  186.5 19.5 %convolution_bitcast_fusion = f32[3072,1536]{0,1:T(8,128)} fusion(f32[192,1536]{1,0:T(8,128)S(1)} %fusion.2, f32[192,3072]{1,0:T(8,128)} %all-gather.8.cloned.1.call-done), kind=kOutput, calls=%fused_computation | convolution fusion | flops 10871635968 | bytes 22413312 | tf_op jit(solution)/shard_map/dot_general | solution.py:18
  206.0 18.7 %copy.23 = f32[3072,1536]{1,0:T(8,128)} copy(f32[3072,1536]{0,1:T(8,128)} %convolution_bitcast_fusion) | data formatting | bytes 37748736
  224.7 0.0 copy-start.3
  224.7 0.0 reduce-scatter.7.cloned.1.call-update
  224.7 0.3 all-gather.10.cloned.1.call-start
  225.0 1.0 copy-done.3
  226.0 0.5 copy.17
  226.4 1.7 copy.19
  228.2 190.7 %reduce-scatter.7.cloned.1.call-done = f32[192,1536]{1,0:T(8,128)} async-done(((f32[3072,1536]{1,0:T(8,128)}), f32[192,1536]{1,0:T(8,128)}) %reduce-scatter.7.cloned.1.call-update) | async-done | bytes 1179664
  418.9 3.0 copy.24
  421.9 4.1 add_divide_fusion
  426.0 0.0 copy-start
  426.0 3.0 copy.20
  429.0 0.0 all-gather.10.cloned.1.call-update
  429.1 0.0 reduce-scatter.5.cloned.1.call-start
  429.1 98.1 %all-gather.10.cloned.1.call-done = f32[3072,1536]{1,0:T(8,128)} async-done(((f32[192,1536]{1,0:T(8,128)}), f32[3072,1536]{1,0:T(8,128)}) %all-gather.10.cloned.1.call-update) | async-done | bytes 18874384 | tf_op jit(solution)/shard_map/all_gather | solution.py:51
  527.2 0.0 copy-done
  527.2 16.5 %fusion.3 = f32[1536,192]{0,1:T(8,128)S(1)} fusion(f32[3072,1536]{1,0:T(8,128)} %all-gather.10.cloned.1.call-done, f32[192,3072]{1,0:T(8,128)S(1)} %copy-done), kind=kOutput, calls=%fused_computation.6 | convolution fusion | flops 10871635968 | bytes 22413312 | tf_op jit(solution)/shard_map/dot_general | solution.py:14
  543.8 23.1 %fusion.4 = f32[192,3072]{1,0:T(8,128)} fusion(f32[1536,192]{0,1:T(8,128)S(1)} %fusion.3, f32[3072,1536]{1,0:T(8,128)} %all-gather.6.cloned.1.call-done), kind=kOutput, calls=%fused_computation.7 | convolution fusion | flops 10871635968 | bytes 22413312 | tf_op jit(solution)/shard_map/dot_general | solution.py:18
  566.9 0.0 copy-start.2
  566.9 0.0 reduce-scatter.5.cloned.1.call-update
  566.9 0.0 copy-start.1
  567.0 1.4 copy-done.2
  568.3 1.5 copy.21
  569.8 0.0 copy-done.1
  569.8 1.5 copy.22
  571.3 30.6 %reduce-scatter.5.cloned.1.call-done = f32[192,1536]{1,0:T(8,128)} async-done(((f32[192,3072]{1,0:T(8,128)}), f32[192,1536]{1,0:T(8,128)}) %reduce-scatter.5.cloned.1.call-update) | async-done | bytes 1179664 | tf_op jit(solution)/shard_map/reduce_scatter | solution.py:53
Async XLA Ops:
  7.2 41.2 %all-gather.12.cloned.1.call-start = ((), (), s32[]{:S(2)}) async-start(), calls=%async_computation.6 | async-start | bytes 3538944 | tf_op jit(solution)/shard_map/all_gather | solution.py:30
  7.9 140.9 %all-gather.6.cloned.1.call-start = ((), (), s32[]{:S(2)}) async-start(), calls=%async_computation.2 | async-start | bytes 20054016 | tf_op jit(solution)/shard_map/all_gather | solution.py:38
  8.6 177.8 %all-gather.8.cloned.1.call-start = ((), (), s32[]{:S(2)}) async-start(), calls=%async_computation.3 | async-start | bytes 3538944 | tf_op jit(solution)/shard_map/all_gather | solution.py:35
  9.4 409.5 %reduce-scatter.7.cloned.1.call-start = ((), (), s32[]{:S(2)}) async-start(), calls=%async_computation.7 | async-start | bytes 20054016
  224.7 1.3 copy-start.3
  224.7 302.5 %all-gather.10.cloned.1.call-start = ((), (), s32[]{:S(2)}) async-start(), calls=%async_computation.4 | async-start | bytes 20054016 | tf_op jit(solution)/shard_map/all_gather | solution.py:51
  426.0 101.2 %copy-start = (f32[192,3072]{1,0:T(8,128)S(1)}, f32[192,3072]{1,0:T(8,128)}, u32[]{:S(2)}) copy-start(f32[192,3072]{1,0:T(8,128)} %all-gather.8.cloned.1.call-done) | copy-start | bytes 7077892
  429.1 172.8 %reduce-scatter.5.cloned.1.call-start = ((), (), s32[]{:S(2)}) async-start(), calls=%async_computation.5 | async-start | bytes 3538944 | tf_op jit(solution)/shard_map/reduce_scatter | solution.py:53
  566.9 1.4 copy-start.2
  566.9 2.9 copy-start.1
Sparse Core Ops, SparseCore 0:
  9.5 38.7 all-gather.11
  49.9 98.8 all-gather.5
  150.4 36.0 all-gather.7
  224.9 194.0 reduce-scatter.6
  429.2 98.0 all-gather.9
  567.1 34.7 reduce-scatter.4
